TPU v7x, 32 devices: a whole 2x2x4 slice. The times are simulated.
32 devices in a mesh: aa: 8 (over z, y), ba: 4 (over x, core).
Axes of the slice: x: 2, y: 2, z: 4, core: 2. Of those that a mesh axis runs over, the one named last changes fastest.
Arguments:
- tokens: bfloat16 [4096, 8192], P('aa', 'ba'), may hold values from -6 to 6
- request_adapter_index: int32 [4096, 1], P('aa'), may hold values from 0 to 127; in each aligned block of 512 rows (0 to 511, 512 to 1023, ...) at most 8 rows name the same one
- key_weight: bfloat16 [8192, 1024], P('ba'), may hold values from -0.0625 to 0.0625
- value_weight: bfloat16 [8192, 1024], P('ba'), may hold values from -0.0625 to 0.0625
- adapter_down_weight: bfloat16 [128, 32, 8192], P('aa', None, 'ba'), may hold values from -0.0625 to 0.0625
- adapter_up_weight: bfloat16 [128, 2, 16, 1024], P('aa'), may hold values from -1.5 to 1.5
Outputs:
- keys_out: bfloat16 [4096, 1024], P('aa', 'ba')
- values_out: bfloat16 [4096, 1024], P('aa', 'ba')
Inputs may be any that keep to these rules, and one draw needn't show every extreme that they name: `request_adapter_index`: among the 512 rows of one device no adapter is named more than 8 times, a bound that some block reaches.
All inputs are finite; a program needn't handle non-finite values.
Results may differ from a plain program's by a relative error of at most 0.001.
Values may be sent and summed in bfloat16 or wider, within the bound.
A program may use at most 128 MiB of HBM per device.

v0:
```python
import functools

import jax
import jax.numpy as jnp
from jax import lax
from jax.experimental import pallas as pl
from jax.experimental.pallas import tpu as pltpu
from jax.sharding import PartitionSpec as P

MESH = pl.DeviceIdType.MESH
LANES = 128
BF16 = jnp.bfloat16
F32 = jnp.float32


def split_two(x):
    hi = x.astype(BF16)
    return hi, (x - hi.astype(F32)).astype(BF16)


def kernel(
    n, m, cap, resident, twice_rank,
    idx_row, tok_hbm, kw_hbm, vw_hbm, down_hbm, up_hbm,
    acc,
    tok, kw, vw, down, up_all, outgoing, recv, rs_send, rs_recv,
    rank_part, rank_in, ret_send, ret_recv,
    load_sem, up_send_sem, up_recv_sem, d_send_sem, d_recv_sem,
    rs_send_sem, rs_recv_sem, p_send_sem, p_recv_sem, r_send_sem, r_recv_sem,
):
    me = lax.axis_index("aa")
    mb = lax.axis_index("ba")
    rows = tok.shape[0]
    kv = acc.shape[1] // 2
    groups = LANES // twice_rank
    quads = resident // groups
    stride = cap * quads
    chunk = resident * cap
    rank = twice_rank // 2

    loads = [
        pltpu.make_async_copy(tok_hbm, tok, load_sem.at[0]),
        pltpu.make_async_copy(
            up_hbm.at[:, pl.ds(pl.multiple_of(mb * kv, LANES), kv)], up_all.at[me], load_sem.at[1]
        ),
        pltpu.make_async_copy(kw_hbm, kw, load_sem.at[2]),
        pltpu.make_async_copy(vw_hbm, vw, load_sem.at[3]),
        pltpu.make_async_copy(down_hbm, down, load_sem.at[4]),
    ]
    for c in loads:
        c.start()

    barrier = pltpu.get_barrier_semaphore()

    def greet_aa(i, _):
        pl.semaphore_signal(barrier, inc=1, device_id={"aa": lax.rem(me + i, n)}, device_id_type=MESH)
        return 0

    def greet_ba(i, _):
        pl.semaphore_signal(barrier, inc=1, device_id={"ba": lax.rem(mb + i, m)}, device_id_type=MESH)
        return 0

    lax.fori_loop(1, n, greet_aa, 0)
    lax.fori_loop(1, m, greet_ba, 0)

    def slot(a, earlier):
        local = lax.rem(a, resident)
        return (a // resident) * chunk + lax.rem(local, groups) * stride + earlier * quads + local // groups

    row = idx_row[...]
    down_pos = lax.broadcasted_iota(jnp.int32, (rows, rows), 0)
    lane_pos = lax.broadcasted_iota(jnp.int32, (rows, rows), 1)
    col = jnp.sum(jnp.where(down_pos == lane_pos, row, 0), axis=1, keepdims=True)
    same = col == row
    slot_col = slot(col, jnp.sum(jnp.where(same & (lane_pos < down_pos), 1, 0), axis=1, keepdims=True))
    slot_row = slot(row, jnp.sum(jnp.where(same & (down_pos < lane_pos), 1, 0), axis=0, keepdims=True))

    def flip(x, b):
        return x + b - 2 * b * lax.rem(x // b, 2)

    bits = []
    bit = n // 2
    while bit:
        bits.append(bit)
        bit //= 2

    far = list(range(n // 2, n))
    near = list(range(n // 4, n // 2))
    order = [0]
    while far:
        if near:
            order.append(near.pop(0))
        order.append(far.pop(0))
    order += near + [d for d in range(n // 4 - 1, 0, -1)]

    def peer(i):
        mask = sum([jnp.where(i == at, order[at], 0) for at in range(1, n)], jnp.int32(0))
        other = me
        for b in bits:
            other = jnp.where(lax.rem(mask // b, 2) == 1, flip(other, b), other)
        return other

    def dispatch(i):
        return pltpu.make_async_remote_copy(
            src_ref=outgoing.at[i], dst_ref=recv.at[i],
            send_sem=d_send_sem.at[i], recv_sem=d_recv_sem.at[i],
            device_id={"aa": peer(i)}, device_id_type=MESH,
        )

    def fill(i):
        wanted = lax.broadcasted_iota(jnp.int32, (chunk, rows), 0) + peer(i) * chunk
        pick = jnp.where(wanted == slot_row, 1.0, 0.0).astype(BF16)
        return jnp.dot(pick, tok[...], preferred_element_type=F32).astype(BF16)

    up_copies = []
    held = [()]
    number = 0
    for b in bits:
        stage = []
        for path in held:
            block = me
            for q in path:
                block = flip(block, q)
            stage.append((block, flip(me, b), number))
            number += 1
        up_copies.append(stage)
        held = held + [path + (b,) for path in held]

    def up_copy(block, partner, at):
        return pltpu.make_async_remote_copy(
            src_ref=up_all.at[block], dst_ref=up_all.at[block],
            send_sem=up_send_sem.at[at], recv_sem=up_recv_sem.at[at],
            device_id={"aa": partner}, device_id_type=MESH,
        )

    pl.semaphore_wait(barrier, n + m - 2)
    loads[1].wait()
    loads[0].wait()

    def send_one(i, _):
        outgoing[i] = fill(i)
        dispatch(i).start()
        return 0

    def up_stage(at):
        if at > 0:
            for entry in up_copies[at - 1]:
                up_copy(*entry).wait_recv()
        if at < len(up_copies):
            for entry in up_copies[at]:
                up_copy(*entry).start()

    up_stage(0)
    lax.fori_loop(1, 3, send_one, 0)

    loads[2].wait()
    loads[3].wait()

    def rs_copy(b):
        return pltpu.make_async_remote_copy(
            src_ref=rs_send.at[b], dst_ref=rs_recv.at[b],
            send_sem=rs_send_sem.at[b], recv_sem=rs_recv_sem.at[b],
            device_id={"ba": lax.rem(mb + b + 1, m)}, device_id_type=MESH,
        )

    def base(b, _):
        cols = pl.ds(pl.multiple_of(lax.rem(mb + b + 1, m) * kv, LANES), kv)
        rs_send[b, :, :kv] = jnp.dot(tok[...], kw[:, cols], preferred_element_type=F32)
        rs_send[b, :, kv:] = jnp.dot(tok[...], vw[:, cols], preferred_element_type=F32)

        @pl.when(b < m - 1)
        def _():
            rs_copy(b).start()

        return 0

    lax.fori_loop(0, m // 2, base, 0)
    up_stage(1)
    lax.fori_loop(3, 5, send_one, 0)
    lax.fori_loop(m // 2, m, base, 0)
    recv[0] = fill(0)
    up_stage(2)
    lax.fori_loop(5, n, send_one, 0)
    loads[4].wait()

    def add_part(b, _):
        rs_copy(b).wait_recv()
        rs_send[m - 1] += rs_recv[b]
        return 0

    width = resident * twice_rank
    slot_of_row = lax.broadcasted_iota(jnp.int32, (chunk, width), 0)
    column = lax.broadcasted_iota(jnp.int32, (chunk, width), 1)
    adapter_of_row = lax.rem(slot_of_row, quads) * groups + slot_of_row // stride
    own = adapter_of_row == column // twice_rank
    for_key = lax.rem(column, twice_rank) < rank

    def part_copy(b, i):
        return pltpu.make_async_remote_copy(
            src_ref=rank_part.at[i], dst_ref=rank_in.at[b, i],
            send_sem=p_send_sem.at[b, i], recv_sem=p_recv_sem.at[b, i],
            device_id={"ba": lax.rem(mb + b + 1, m)}, device_id_type=MESH,
        )

    def ret_copy(i):
        return pltpu.make_async_remote_copy(
            src_ref=ret_send.at[i], dst_ref=ret_recv.at[i],
            send_sem=r_send_sem.at[i], recv_sem=r_recv_sem.at[i],
            device_id={"aa": peer(i)}, device_id_type=MESH,
        )

    def partial(i):
        @pl.when(i > 0)
        def _():
            dispatch(i).wait_recv()

        wide = lax.dot_general(
            recv[i], down[...], (((1,), (1,)), ((), ())), preferred_element_type=F32
        )
        wide = jnp.where(own, wide, 0.0)
        total = wide[:, :LANES]
        for q in range(1, width // LANES):
            total = total + wide[:, q * LANES:(q + 1) * LANES]
        packed = total[:stride]
        for g in range(1, groups):
            packed = packed + total[g * stride:(g + 1) * stride]
        rank_part[i] = packed
        for b in range(m - 1):
            part_copy(b, i).start()

    def finish(i):
        total = rank_part[i]
        for b in range(m - 1):
            part_copy(b, i).wait_recv()
            total = total + rank_in[b, i]

        @pl.when(i == 0)
        def _():
            ret_recv[i] = total

        @pl.when(i > 0)
        def _():
            ret_send[i] = total
            ret_copy(i).start()

    def final(i):
        @pl.when(i > 0)
        def _():
            ret_copy(i).wait_recv()

        tall = jnp.concatenate([ret_recv[i]] * groups, axis=0)
        spread = jnp.where(own, jnp.concatenate([tall] * (width // LANES), axis=1), 0.0)
        key_hi, key_lo = split_two(jnp.where(for_key, spread, 0.0))
        value_hi, value_lo = split_two(jnp.where(for_key, 0.0, spread))
        bank = peer(i)
        up = up_all[bank]
        pieces = jnp.concatenate([key_hi, key_lo, value_hi, value_lo], axis=0)
        out = jnp.dot(pieces, up, preferred_element_type=F32)
        change = jnp.concatenate(
            [out[:chunk] + out[chunk:2 * chunk], out[2 * chunk:3 * chunk] + out[3 * chunk:]], axis=1
        )
        hi, lo = split_two(change)
        place = lax.broadcasted_iota(jnp.int32, (rows, chunk), 1) + bank * chunk
        pick = jnp.where(place == slot_col, 1.0, 0.0).astype(BF16)
        acc[...] += jnp.dot(pick, hi, preferred_element_type=F32) + jnp.dot(
            pick, lo, preferred_element_type=F32
        )

    def step(t, _):
        @pl.when((t >= 1) & (t < n + 1))
        def _():
            finish(t - 1)

        @pl.when(t == 2)
        def _():
            for at in range(3, len(up_copies) + 1):
                up_stage(at)
            lax.fori_loop(0, m - 1, add_part, 0)
            acc[...] = rs_send[m - 1]

        @pl.when(t >= 2)
        def _():
            final(t - 2)

        @pl.when(t < n)
        def _():
            partial(t)

        return 0

    lax.fori_loop(0, n + 2, step, 0)

    for stage in up_copies:
        for entry in stage:
            up_copy(*entry).wait_send()

    def drain(i, _):
        dispatch(i).wait_send()
        ret_copy(i).wait_send()
        return 0

    lax.fori_loop(1, n, drain, 0)

    def drain_parts(i, _):
        for b in range(m - 1):
            part_copy(b, i).wait_send()
        return 0

    lax.fori_loop(0, n, drain_parts, 0)
    for b in range(m - 1):
        rs_copy(b).wait_send()


def on_device(n, m, tokens, request_adapter_index, key_weight, value_weight, down_weight, up_weight):
    rows, width = tokens.shape
    resident, twice_rank, _ = down_weight.shape
    kv_width = key_weight.shape[1]
    kv = kv_width // m
    cap = max(2, 2 * rows // (resident * n))
    chunk = resident * cap
    packed = chunk * twice_rank // LANES
    flat = resident * twice_rank
    dma = pltpu.SemaphoreType.DMA
    total = pl.pallas_call(
        functools.partial(kernel, n, m, cap, resident, twice_rank),
        out_shape=jax.ShapeDtypeStruct((rows, 2 * kv), F32),
        in_specs=[pl.BlockSpec(memory_space=pltpu.VMEM)] + [pl.BlockSpec(memory_space=pl.ANY)] * 5,
        out_specs=pl.BlockSpec(memory_space=pltpu.VMEM),
        scratch_shapes=[
            pltpu.VMEM((rows, width), BF16),
            pltpu.VMEM((width, kv_width), BF16),
            pltpu.VMEM((width, kv_width), BF16),
            pltpu.VMEM((flat, width), BF16),
            pltpu.VMEM((n, flat, kv), BF16),
            pltpu.VMEM((n, chunk, width), BF16),
            pltpu.VMEM((n, chunk, width), BF16),
            pltpu.VMEM((m, rows, 2 * kv), F32),
            pltpu.VMEM((m - 1, rows, 2 * kv), F32),
            pltpu.VMEM((n, packed, LANES), F32),
            pltpu.VMEM((m - 1, n, packed, LANES), F32),
            pltpu.VMEM((n, packed, LANES), F32),
            pltpu.VMEM((n, packed, LANES), F32),
            dma((5,)),
            dma((n,)), dma((n,)), dma((n,)), dma((n,)),
            dma((m,)), dma((m,)),
            dma((m - 1, n)), dma((m - 1, n)),
            dma((n,)), dma((n,)),
        ],
        compiler_params=pltpu.CompilerParams(
            collective_id=0, has_side_effects=True, vmem_limit_bytes=56 * 1024 * 1024
        ),
    )(
        request_adapter_index.reshape(1, rows),
        tokens,
        key_weight,
        value_weight,
        down_weight.reshape(flat, width),
        up_weight.reshape(flat, kv_width),
    )
    return total[:, :kv].astype(BF16), total[:, kv:].astype(BF16)


def solution(mesh):
    return jax.shard_map(
        functools.partial(on_device, mesh.shape["aa"], mesh.shape["ba"]),
        mesh=mesh,
        in_specs=(
            P("aa", "ba"),
            P("aa", None),
            P("ba", None),
            P("ba", None),
            P("aa", None, "ba"),
            P("aa", None, None, None),
        ),
        out_specs=(P("aa", "ba"), P("aa", "ba")),
        check_vma=False,
    )
```

profile of v0, /device:TPU:0, one launch (start us, length us, event | category | flops | bytes accessed | tf_op | source)
XLA Modules:
  0.0 139.5 jit_solution(2530496278011542233)
XLA Ops:
  0.6 136.7 %shard_map.77 = f32[512,512]{1,0:T(8,128)} custom-call(s32[1,512]{1,0:T(1,128)} %bitcast.5, bf16[512,2048]{1,0:T(8,128)(2,1)} %tok_hbm.1, bf16[2048,1024]{1,0:T(8,128)(2,1)} %kw_hbm.1, bf16[2048,1024]{1,0:T(8,128)(2,1)} %vw_hbm.1, bf16[512,2048]{1,0:T(8,128)(2,1)} %bitcast.3, bf16[512,1024]{1,0:T(8,128)(2,1)} %bitcast.4), custom_call_target="tpu_custom_call" | custom-call | tf_op jit(solution)/shard_map/pallas_call | solution.py:323
  137.4 1.3 convert.4
  138.7 0.8 fusion
where the time goes:
time: 140 us
  Pallas kernels  137 us (98%)
    pallas_call x1, Pallas kernels, on_device(): pl.pallas_call(functools.partial(kernel, n, m, cap, resident, twice_rank)...  137 us

commit v1 on v0

--- a/solution.py
+++ b/solution.py
@@ -310,6 +310,488 @@
         rs_copy(b).wait_send()
 
 
+def xor_bit(x, b):
+    return x + b - 2 * b * lax.rem(x // b, 2)
+
+
+def bits_of(count):
+    found = []
+    bit = count // 2
+    while bit:
+        found.append(bit)
+        bit //= 2
+    return found
+
+
+def low_bit(mask):
+    return mask & -mask
+
+
+def packed_kernel(
+    n, m, direct, shared, near_rows, stride, resident, twice_rank,
+    idx_hbm, tok_hbm, kw_hbm, vw_hbm, down_hbm, up_hbm,
+    keys, values, flag,
+    idx_mine, idx_all, mine, tri, tok, kw, vw, down, up_all, shared_out, outgoing, recv,
+    rs_send, rs_recv, acc, rank_part, rank_in, ret_send, ret_recv,
+    load_sem, idx_send_sem, idx_recv_sem, up_send_sem, up_recv_sem, v_send_sem, v_recv_sem,
+    d_send_sem, d_recv_sem, rs_send_sem, rs_recv_sem, p_send_sem, p_recv_sem, r_send_sem, r_recv_sem,
+):
+    me = lax.axis_index("aa")
+    mb = lax.axis_index("ba")
+    rows = tok.shape[0]
+    kv = keys.shape[1]
+    half = n // 2
+    slots = direct + shared
+    groups = LANES // twice_rank
+    packed = rank_part.shape[1]
+    rank = twice_rank // 2
+    width = resident * twice_rank
+    bits = bits_of(n)
+    ba_bits = bits_of(m)[::-1]
+    count = jnp.int32
+
+    barrier = pltpu.get_barrier_semaphore()
+
+    def greet_aa(i, _):
+        pl.semaphore_signal(barrier, inc=1, device_id={"aa": lax.rem(me + i, n)}, device_id_type=MESH)
+        return 0
+
+    def greet_ba(i, _):
+        pl.semaphore_signal(barrier, inc=1, device_id={"ba": lax.rem(mb + i, m)}, device_id_type=MESH)
+        return 0
+
+    lax.fori_loop(1, n, greet_aa, 0)
+    lax.fori_loop(1, m, greet_ba, 0)
+
+    loads = [
+        pltpu.make_async_copy(idx_hbm, idx_mine, load_sem.at[0]),
+        pltpu.make_async_copy(
+            up_hbm.at[:, pl.ds(pl.multiple_of(mb * kv, LANES), kv)], up_all.at[0], load_sem.at[1]
+        ),
+        pltpu.make_async_copy(tok_hbm, tok, load_sem.at[2]),
+        pltpu.make_async_copy(kw_hbm, kw, load_sem.at[3]),
+        pltpu.make_async_copy(vw_hbm, vw, load_sem.at[4]),
+        pltpu.make_async_copy(down_hbm, down, load_sem.at[5]),
+    ]
+    for c in loads:
+        c.start()
+
+    def partner(mask):
+        other = me
+        for b in bits:
+            other = jnp.where(lax.rem(mask // b, 2) == 1, xor_bit(other, b), other)
+        return other
+
+    def chosen(masks, t):
+        return sum([jnp.where(t == at, mask, 0) for at, mask in enumerate(masks)], jnp.int32(0))
+
+    def idx_copy(mask, source):
+        return pltpu.make_async_remote_copy(
+            src_ref=idx_mine, dst_ref=idx_all.at[source],
+            send_sem=idx_send_sem.at[mask], recv_sem=idx_recv_sem.at[mask],
+            device_id={"aa": partner(mask)}, device_id_type=MESH,
+        )
+
+    def up_copy(mask):
+        hop = low_bit(mask)
+        return pltpu.make_async_remote_copy(
+            src_ref=up_all.at[mask - hop], dst_ref=up_all.at[mask],
+            send_sem=up_send_sem.at[mask], recv_sem=up_recv_sem.at[mask],
+            device_id={"aa": xor_bit(me, hop)}, device_id_type=MESH,
+        )
+
+    def shared_copy(mask):
+        hop = low_bit(mask)
+        source = shared_out if mask == half else recv.at[mask - hop, pl.ds(direct, shared)]
+        return pltpu.make_async_remote_copy(
+            src_ref=source, dst_ref=recv.at[mask, pl.ds(direct, shared)],
+            send_sem=v_send_sem.at[mask], recv_sem=v_recv_sem.at[mask],
+            device_id={"aa": xor_bit(me, hop)}, device_id_type=MESH,
+        )
+
+    def row_copy(mask, height):
+        return pltpu.make_async_remote_copy(
+            src_ref=outgoing.at[mask, pl.ds(0, height)], dst_ref=recv.at[mask, pl.ds(0, height)],
+            send_sem=d_send_sem.at[mask], recv_sem=d_recv_sem.at[mask],
+            device_id={"aa": partner(mask)}, device_id_type=MESH,
+        )
+
+    def hops_below(mask):
+        return [b for b in bits if b < low_bit(mask)]
+
+    earlier = lax.broadcasted_iota(count, (rows, rows), 0)
+    later = lax.broadcasted_iota(count, (rows, rows), 1)
+    tri[...] = jnp.where(earlier < later, 1.0, 0.0).astype(BF16)
+    loads[0].wait()
+    row = idx_mine[...]
+    bank_row = row // resident
+    tall = max(16, n)
+    match = lax.broadcasted_iota(count, (tall, rows), 0) == bank_row
+    ranks = jnp.dot(jnp.where(match, 1.0, 0.0).astype(BF16), tri[...], preferred_element_type=F32)
+    rank_row = jnp.sum(jnp.where(match, ranks, 0.0), axis=0, keepdims=True).astype(count)
+    far_row = (bank_row // half) != (me // half)
+    over_row = jnp.where(far_row & (rank_row >= direct), 1.0, 0.0)
+    over_rank = jnp.dot(
+        jnp.broadcast_to(over_row, (tall, rows)).astype(BF16), tri[...], preferred_element_type=F32
+    )[:1].astype(count)
+    slot_row = jnp.where(over_row > 0.5, direct + over_rank, rank_row)
+    code_row = bank_row * stride + slot_row
+    shared_row = jnp.where(over_row > 0.5, over_rank, -1)
+
+    def gathered(wanted, at):
+        pick = jnp.where(wanted == at, 1.0, 0.0).astype(BF16)
+        return jnp.dot(pick, tok[...], preferred_element_type=F32).astype(BF16)
+
+    def fill(bank, height):
+        return gathered(lax.broadcasted_iota(count, (height, rows), 0) + bank * stride, code_row)
+
+    pl.semaphore_wait(barrier, n + m - 2)
+
+    def send_idx(mask, _):
+        idx_copy(mask, me).start()
+        return 0
+
+    lax.fori_loop(1, n, send_idx, 0)
+    loads[1].wait()
+    for b in bits:
+        if b != half // 2:
+            up_copy(b).start()
+    loads[2].wait()
+    shared_out[...] = gathered(lax.broadcasted_iota(count, (shared, rows), 0), shared_row)
+    shared_copy(half).start()
+    if half > 1:
+        up_copy(half // 2).start()
+
+    near = sorted(range(1, half), key=lambda mask: (-low_bit(mask) * 0 - mask // 2, mask))
+    far = sorted(range(half, n), key=lambda mask: (mask % 2, mask))
+
+    def send_near(t, _):
+        mask = chosen(near, t)
+        outgoing[mask] = fill(partner(mask), near_rows)
+        row_copy(mask, near_rows).start()
+        return 0
+
+    def send_far(t, _):
+        mask = chosen(far, t)
+        outgoing[mask, pl.ds(0, direct)] = fill(partner(mask), direct)
+        row_copy(mask, direct).start()
+        return 0
+
+    lax.fori_loop(0, len(near), send_near, 0)
+    first = len(far) // 2
+    lax.fori_loop(0, first, send_far, 0)
+
+    def rs_copy(q):
+        hop = low_bit(q)
+        return pltpu.make_async_remote_copy(
+            src_ref=rs_send.at[q], dst_ref=rs_recv.at[q],
+            send_sem=rs_send_sem.at[q], recv_sem=rs_recv_sem.at[q],
+            device_id={"ba": xor_bit(mb, hop)}, device_id_type=MESH,
+        )
+
+    loads[3].wait()
+    loads[4].wait()
+    base_order = sorted(range(1, m), key=lambda q: (low_bit(q), q)) + [0]
+
+    def base(t, _):
+        q = chosen(base_order, t)
+        block = mb
+        for b in ba_bits:
+            block = jnp.where(lax.rem(q // b, 2) == 1, xor_bit(block, b), block)
+        cols = pl.ds(pl.multiple_of(block * kv, LANES), kv)
+        rs_send[q, :, :kv] = jnp.dot(tok[...], kw[:, cols], preferred_element_type=F32)
+        rs_send[q, :, kv:] = jnp.dot(tok[...], vw[:, cols], preferred_element_type=F32)
+        for at, q_now in enumerate(base_order):
+            if q_now:
+                @pl.when(t == at)
+                def _():
+                    for b in ba_bits:
+                        if b < low_bit(q_now):
+                            rs_copy(q_now + b).wait_recv()
+                            rs_send[q_now] += rs_recv[q_now + b]
+                    rs_copy(q_now).start()
+
+        return 0
+
+    lax.fori_loop(0, m, base, 0)
+
+    idx_all[me] = row
+    for_self = fill(me, near_rows)
+    recv[0, pl.ds(0, near_rows)] = for_self
+    for mask in range(half):
+        recv[mask, pl.ds(near_rows, slots - near_rows)] = jnp.zeros((slots - near_rows, tok.shape[1]), BF16)
+
+    def wait_idx(mask, _):
+        idx_copy(mask, partner(mask)).wait_recv()
+        return 0
+
+    lax.fori_loop(1, n, wait_idx, 0)
+    everyone = jnp.concatenate([idx_all[s] for s in range(n)], axis=0)
+    banks = everyone // resident
+    matches = [banks == b for b in range(n)]
+    stacked = jnp.concatenate([jnp.where(hit, 1.0, 0.0) for hit in matches], axis=0)
+    all_ranks = jnp.dot(stacked.astype(BF16), tri[...], preferred_element_type=F32)
+    place = jnp.zeros((n, rows), F32)
+    for b in range(n):
+        place = place + jnp.where(matches[b], all_ranks[b * n:(b + 1) * n], 0.0)
+    place = place.astype(count)
+    far_all = (banks // half) != (lax.broadcasted_iota(count, (n, rows), 0) // half)
+    over_all = jnp.where(far_all & (place >= direct), 1.0, 0.0)
+    padded = jnp.concatenate([over_all] * (tall // n), axis=0)
+    over_ranks = jnp.dot(padded.astype(BF16), tri[...], preferred_element_type=F32)[:n].astype(count)
+    place = jnp.where(over_all > 0.5, direct + over_ranks, place)
+    excess = jnp.where(place >= jnp.where(far_all, slots, near_rows), 1, 0)
+    flag[...] = jnp.broadcast_to(
+        jnp.max(jnp.max(excess, axis=1, keepdims=True), axis=0, keepdims=True), flag.shape
+    )
+    to_me = jnp.where(banks == me, place, -1)
+    for s in range(n):
+        mine[s] = to_me[s:s + 1]
+    code_col = jnp.sum(jnp.where(earlier == later, code_row, 0), axis=1, keepdims=True)
+
+    lane = lax.broadcasted_iota(count, (packed, LANES), 1) // twice_rank
+    column = lax.broadcasted_iota(count, (slots, width), 1)
+    for_key = lax.rem(column, twice_rank) < rank
+
+    def folded(x):
+        total = x
+        for g in range(1, groups):
+            total = total + pltpu.roll(x, g * twice_rank, axis=1)
+        return total
+
+    def owned(wanted, at, ids):
+        local = jnp.sum(jnp.where(wanted == at, lax.rem(ids, resident), 0), axis=1, keepdims=True)
+        return local == column // twice_rank
+
+    def part_copy(b, mask):
+        return pltpu.make_async_remote_copy(
+            src_ref=rank_part.at[mask], dst_ref=rank_in.at[b, mask],
+            send_sem=p_send_sem.at[b, mask], recv_sem=p_recv_sem.at[b, mask],
+            device_id={"ba": lax.rem(mb + b + 1, m)}, device_id_type=MESH,
+        )
+
+    def ret_copy(mask):
+        return pltpu.make_async_remote_copy(
+            src_ref=ret_send.at[mask], dst_ref=ret_recv.at[mask],
+            send_sem=r_send_sem.at[mask], recv_sem=r_recv_sem.at[mask],
+            device_id={"aa": partner(mask)}, device_id_type=MESH,
+        )
+
+    def partial(mask):
+        @pl.when((mask > 0) & (mask < half))
+        def _():
+            row_copy(mask, near_rows).wait_recv()
+
+        @pl.when(mask >= half)
+        def _():
+            row_copy(mask, direct).wait_recv()
+
+        source = partner(mask)
+        wide = lax.dot_general(
+            recv[mask], down[...], (((1,), (1,)), ((), ())), preferred_element_type=F32
+        )
+        own = owned(lax.broadcasted_iota(count, (slots, rows), 0), mine[source], idx_all[source])
+        wide = jnp.where(own, wide, 0.0)
+        total = wide[:, :LANES]
+        for q in range(1, width // LANES):
+            total = total + wide[:, q * LANES:(q + 1) * LANES]
+        total = folded(total)
+        if groups * packed > slots:
+            total = jnp.concatenate([total, jnp.zeros((groups * packed - slots, LANES), F32)], axis=0)
+        together = total[:packed]
+        for g in range(1, groups):
+            together = jnp.where(lane == g, total[g * packed:(g + 1) * packed], together)
+        rank_part[mask] = together
+        for b in range(m - 1):
+            part_copy(b, mask).start()
+
+    def finish(mask):
+        total = rank_part[mask]
+        for b in range(m - 1):
+            part_copy(b, mask).wait_recv()
+            total = total + rank_in[b, mask]
+
+        @pl.when(mask == 0)
+        def _():
+            ret_recv[mask] = total
+
+        @pl.when(mask > 0)
+        def _():
+            ret_send[mask] = total
+            ret_copy(mask).start()
+
+    def final(mask):
+        @pl.when(mask > 0)
+        def _():
+            ret_copy(mask).wait_recv()
+
+        bank = partner(mask)
+        together = ret_recv[mask]
+        tall_ranks = jnp.concatenate(
+            [folded(jnp.where(lane == g, together, 0.0)) for g in range(groups)], axis=0
+        )[:slots]
+        own = owned(lax.broadcasted_iota(count, (slots, rows), 0) + bank * stride, code_row, row)
+        spread = jnp.where(own, jnp.concatenate([tall_ranks] * (width // LANES), axis=1), 0.0)
+        key_hi, key_lo = split_two(jnp.where(for_key, spread, 0.0))
+        value_hi, value_lo = split_two(jnp.where(for_key, 0.0, spread))
+        pieces = jnp.concatenate([key_hi, key_lo, value_hi, value_lo], axis=0)
+        out = jnp.dot(pieces, up_all[mask], preferred_element_type=F32)
+        change = jnp.concatenate(
+            [out[:slots] + out[slots:2 * slots], out[2 * slots:3 * slots] + out[3 * slots:]], axis=1
+        )
+        hi, lo = split_two(change)
+        pick = jnp.where(
+            lax.broadcasted_iota(count, (rows, slots), 1) + bank * stride == code_col, 1.0, 0.0
+        ).astype(BF16)
+        acc[...] += jnp.dot(pick, hi, preferred_element_type=F32) + jnp.dot(
+            pick, lo, preferred_element_type=F32
+        )
+
+    order = [0] + sorted(range(1, half), key=lambda mask: (mask // 2, mask)) + far
+    loads[5].wait()
+
+    def relay_up(mask):
+        up_copy(mask).wait_recv()
+        for b in hops_below(mask):
+            up_copy(mask + b).start()
+
+    def relay_shared(mask):
+        shared_copy(mask).wait_recv()
+        for b in hops_below(mask):
+            shared_copy(mask + b).start()
+
+    def step(t, _):
+        @pl.when((t >= 1) & (t < n + 1))
+        def _():
+            finish(chosen(order, t - 1))
+
+        for at, mask in enumerate(order):
+            if mask and mask != half and mask % 2 == 0 or mask > half:
+                @pl.when(t == at)
+                def _():
+                    if mask % 2 == 0:
+                        relay_up(mask)
+                    if mask > half:
+                        relay_shared(mask)
+
+        @pl.when(t == 2)
+        def _():
+            for b in ba_bits:
+                rs_copy(b).wait_recv()
+                rs_send[0] += rs_recv[b]
+            acc[...] = rs_send[0]
+
+        @pl.when(t >= 2)
+        def _():
+            for at, mask in enumerate(order):
+                if mask % 2:
+                    @pl.when(t == at + 2)
+                    def _():
+                        up_copy(mask).wait_recv()
+
+            final(chosen(order, t - 2))
+
+        @pl.when(t < n)
+        def _():
+            partial(chosen(order, t))
+
+        return 0
+
+    lax.fori_loop(0, 2, step, 0)
+    relay_up(half)
+    lax.fori_loop(first, len(far) - 1, send_far, 0)
+    relay_shared(half)
+    lax.fori_loop(len(far) - 1, len(far), send_far, 0)
+    lax.fori_loop(2, n + 2, step, 0)
+    keys[...] = acc[:, :kv].astype(BF16)
+    values[...] = acc[:, kv:].astype(BF16)
+
+    for mask in range(1, n):
+        up_copy(mask).wait_send()
+    for mask in range(half, n):
+        shared_copy(mask).wait_send()
+
+    def drain(mask, _):
+        idx_copy(mask, me).wait_send()
+        ret_copy(mask).wait_send()
+
+        @pl.when(mask < half)
+        def _():
+            row_copy(mask, near_rows).wait_send()
+
+        @pl.when(mask >= half)
+        def _():
+            row_copy(mask, direct).wait_send()
+
+        return 0
+
+    lax.fori_loop(1, n, drain, 0)
+
+    def drain_parts(mask, _):
+        for b in range(m - 1):
+            part_copy(b, mask).wait_send()
+        return 0
+
+    lax.fori_loop(0, n, drain_parts, 0)
+    for q in range(1, m):
+        rs_copy(q).wait_send()
+
+
+def packed_call(n, m, cap, idx, tokens, key_weight, value_weight, down_flat, up_flat, resident):
+    rows, width = tokens.shape
+    flat = down_flat.shape[0]
+    twice_rank = flat // resident
+    kv_width = key_weight.shape[1]
+    kv = kv_width // m
+    direct = rows // n
+    shared = 3 * direct // 4
+    near_rows = 3 * direct // 2
+    slots = direct + shared
+    stride = resident * cap
+    packed = stride * twice_rank // LANES
+    dma = pltpu.SemaphoreType.DMA
+    return pl.pallas_call(
+        functools.partial(packed_kernel, n, m, direct, shared, near_rows, stride, resident, twice_rank),
+        out_shape=[
+            jax.ShapeDtypeStruct((rows, kv), BF16),
+            jax.ShapeDtypeStruct((rows, kv), BF16),
+            jax.ShapeDtypeStruct((8, LANES), jnp.int32),
+        ],
+        in_specs=[pl.BlockSpec(memory_space=pl.ANY)] * 6,
+        out_specs=[pl.BlockSpec(memory_space=pltpu.VMEM)] * 3,
+        scratch_shapes=[
+            pltpu.VMEM((1, rows), jnp.int32),
+            pltpu.VMEM((n, 1, rows), jnp.int32),
+            pltpu.VMEM((n, 1, rows), jnp.int32),
+            pltpu.VMEM((rows, rows), BF16),
+            pltpu.VMEM((rows, width), BF16),
+            pltpu.VMEM((width, kv_width), BF16),
+            pltpu.VMEM((width, kv_width), BF16),
+            pltpu.VMEM((flat, width), BF16),
+            pltpu.VMEM((n, flat, kv), BF16),
+            pltpu.VMEM((shared, width), BF16),
+            pltpu.VMEM((n, near_rows, width), BF16),
+            pltpu.VMEM((n, slots, width), BF16),
+            pltpu.VMEM((m, rows, 2 * kv), F32),
+            pltpu.VMEM((m, rows, 2 * kv), F32),
+            pltpu.VMEM((rows, 2 * kv), F32),
+            pltpu.VMEM((n, packed, LANES), F32),
+            pltpu.VMEM((m - 1, n, packed, LANES), F32),
+            pltpu.VMEM((n, packed, LANES), F32),
+            pltpu.VMEM((n, packed, LANES), F32),
+            dma((6,)),
+            dma((n,)), dma((n,)), dma((n,)), dma((n,)), dma((n,)), dma((n,)),
+            dma((n,)), dma((n,)),
+            dma((m,)), dma((m,)),
+            dma((m - 1, n)), dma((m - 1, n)),
+            dma((n,)), dma((n,)),
+        ],
+        compiler_params=pltpu.CompilerParams(
+            collective_id=1, has_side_effects=True, vmem_limit_bytes=56 * 1024 * 1024
+        ),
+    )(idx, tokens, key_weight, value_weight, down_flat, up_flat)
+
+
 def on_device(n, m, tokens, request_adapter_index, key_weight, value_weight, down_weight, up_weight):
     rows, width = tokens.shape
     resident, twice_rank, _ = down_weight.shape
@@ -319,36 +801,7 @@
     chunk = resident * cap
     packed = chunk * twice_rank // LANES
     flat = resident * twice_rank
-    dma = pltpu.SemaphoreType.DMA
-    total = pl.pallas_call(
-        functools.partial(kernel, n, m, cap, resident, twice_rank),
-        out_shape=jax.ShapeDtypeStruct((rows, 2 * kv), F32),
-        in_specs=[pl.BlockSpec(memory_space=pltpu.VMEM)] + [pl.BlockSpec(memory_space=pl.ANY)] * 5,
-        out_specs=pl.BlockSpec(memory_space=pltpu.VMEM),
-        scratch_shapes=[
-            pltpu.VMEM((rows, width), BF16),
-            pltpu.VMEM((width, kv_width), BF16),
-            pltpu.VMEM((width, kv_width), BF16),
-            pltpu.VMEM((flat, width), BF16),
-            pltpu.VMEM((n, flat, kv), BF16),
-            pltpu.VMEM((n, chunk, width), BF16),
-            pltpu.VMEM((n, chunk, width), BF16),
-            pltpu.VMEM((m, rows, 2 * kv), F32),
-            pltpu.VMEM((m - 1, rows, 2 * kv), F32),
-            pltpu.VMEM((n, packed, LANES), F32),
-            pltpu.VMEM((m - 1, n, packed, LANES), F32),
-            pltpu.VMEM((n, packed, LANES), F32),
-            pltpu.VMEM((n, packed, LANES), F32),
-            dma((5,)),
-            dma((n,)), dma((n,)), dma((n,)), dma((n,)),
-            dma((m,)), dma((m,)),
-            dma((m - 1, n)), dma((m - 1, n)),
-            dma((n,)), dma((n,)),
-        ],
-        compiler_params=pltpu.CompilerParams(
-            collective_id=0, has_side_effects=True, vmem_limit_bytes=56 * 1024 * 1024
-        ),
-    )(
+    operands = (
         request_adapter_index.reshape(1, rows),
         tokens,
         key_weight,
@@ -356,7 +809,46 @@
         down_weight.reshape(flat, width),
         up_weight.reshape(flat, kv_width),
     )
-    return total[:, :kv].astype(BF16), total[:, kv:].astype(BF16)
+
+    def any_load():
+        dma = pltpu.SemaphoreType.DMA
+        total = pl.pallas_call(
+            functools.partial(kernel, n, m, cap, resident, twice_rank),
+            out_shape=jax.ShapeDtypeStruct((rows, 2 * kv), F32),
+            in_specs=[pl.BlockSpec(memory_space=pltpu.VMEM)] + [pl.BlockSpec(memory_space=pl.ANY)] * 5,
+            out_specs=pl.BlockSpec(memory_space=pltpu.VMEM),
+            scratch_shapes=[
+                pltpu.VMEM((rows, width), BF16),
+                pltpu.VMEM((width, kv_width), BF16),
+                pltpu.VMEM((width, kv_width), BF16),
+                pltpu.VMEM((flat, width), BF16),
+                pltpu.VMEM((n, flat, kv), BF16),
+                pltpu.VMEM((n, chunk, width), BF16),
+                pltpu.VMEM((n, chunk, width), BF16),
+                pltpu.VMEM((m, rows, 2 * kv), F32),
+                pltpu.VMEM((m - 1, rows, 2 * kv), F32),
+                pltpu.VMEM((n, packed, LANES), F32),
+                pltpu.VMEM((m - 1, n, packed, LANES), F32),
+                pltpu.VMEM((n, packed, LANES), F32),
+                pltpu.VMEM((n, packed, LANES), F32),
+                dma((5,)),
+                dma((n,)), dma((n,)), dma((n,)), dma((n,)),
+                dma((m,)), dma((m,)),
+                dma((m - 1, n)), dma((m - 1, n)),
+                dma((n,)), dma((n,)),
+            ],
+            compiler_params=pltpu.CompilerParams(
+                collective_id=0, has_side_effects=True, vmem_limit_bytes=56 * 1024 * 1024
+            ),
+        )(
+            *operands,
+        )
+        return total[:, :kv].astype(BF16), total[:, kv:].astype(BF16)
+
+    if rows % (64 * n) or 7 * rows // (4 * n) >= chunk:
+        return any_load()
+    keys, values, flag = packed_call(n, m, cap, *operands, resident)
+    return lax.cond(flag[0, 0] > 0, any_load, lambda: (keys, values))
 
 
 def solution(mesh):

time: 140 us -> 104 us (0.74)
  the two profiles are of different devices: /device:TPU:0 before, /device:TPU:11 now
where the time goes in v1:
time: 104 us; the launch traced here: 102 us
  Pallas kernels  97.6 us (94%)
  local copies, waits for them, and re-layouts  2.62 us (3%)
  between operations  1.36 us (1%)
    pallas_call x1, Pallas kernels, packed_call(): pl.pallas_call(functools.partial(packed_kernel, n, m, direct, shared, nea...  97.6 us

profile of v1, /device:TPU:11, one launch (start us, length us, event | category | flops | bytes accessed | tf_op | source)
XLA Modules:
  0.0 101.8 jit_solution(10604969322899474784)
XLA Ops:
  0.6 0.0 copy-start
  0.6 0.0 copy-start.1
  0.7 0.0 copy-start.2
  0.7 0.0 copy-start.3
  0.7 97.6 %shard_map.81 = (bf16[512,256]{1,0:T(8,128)(2,1)S(1)}, bf16[512,256]{1,0:T(8,128)(2,1)S(1)}, s32[8,128]{1,0:T(8,128)}) custom-call(s32[1,512]{1,0:T(1,128)} %bitcast.8, bf16[512,2048]{1,0:T(8,128)(2,1)} %tok_hbm.1, bf16[2048,1024]{1,0:T(8,128)(2,1)} %kw_hbm.1, bf16[2048,1024]{1,0:T(8,128)(2,1)} %vw_hbm.1, bf16[512,2048]{1,0:T(8,128)(2,1)} %bitcast.4, ...), custom_call_target="tpu_custom_call" | custom-call | tf_op jit(solution)/shard_map/pallas_call | solution.py:753
  98.3 1.2 %slice.11 = s32[1,1]{1,0:T(1,128)} slice(s32[8,128]{1,0:T(8,128)} %get-tuple-element.27), slice={[0:1], [0:1]} | slice | bytes 8 | tf_op jit(solution)/shard_map/slice | solution.py:851
  100.1 0.0 copy-done
  100.1 0.0 copy-done.1
  100.2 0.0 copy-done.2
  100.2 0.0 copy-done.3
  100.2 0.2 conditional.1
  100.4 0.7 copy.18
  101.1 0.7 copy.19
Async XLA Ops:
  0.6 99.5 %copy-start = (bf16[512,2048]{1,0:T(8,128)(2,1)S(1)}, bf16[512,2048]{1,0:T(8,128)(2,1)}, u32[]{:S(2)}) copy-start(bf16[512,2048]{1,0:T(8,128)(2,1)} %tok_hbm.1) | copy-start | bytes 6291460
  0.6 99.5 %copy-start.1 = (bf16[16,32,2048]{2,1,0:T(8,128)(2,1)S(1)}, bf16[16,32,2048]{2,1,0:T(8,128)(2,1)}, u32[]{:S(2)}) copy-start(bf16[16,32,2048]{2,1,0:T(8,128)(2,1)} %param.12) | copy-start | bytes 6291460
  0.7 99.5 %copy-start.2 = (bf16[16,2,16,1024]{3,2,1,0:T(8,128)(2,1)S(1)}, bf16[16,2,16,1024]{3,2,1,0:T(8,128)(2,1)}, u32[]{:S(2)}) copy-start(bf16[16,2,16,1024]{3,2,1,0:T(8,128)(2,1)} %param.13) | copy-start | bytes 3145732
  0.7 99.5 %copy-start.3 = (s32[512,1]{0,1:T(1,128)S(1)}, s32[512,1]{0,1:T(1,128)}, u32[]{:S(2)}) copy-start(s32[512,1]{0,1:T(1,128)} %param.9) | copy-start | bytes 6148

commit v2 on v1

--- a/solution.py
+++ b/solution.py
@@ -330,16 +330,16 @@
 def packed_kernel(
     n, m, direct, shared, near_rows, stride, resident, twice_rank,
     idx_hbm, tok_hbm, kw_hbm, vw_hbm, down_hbm, up_hbm,
-    keys, values, flag,
+    out, flag_hbm,
     idx_mine, idx_all, mine, tri, tok, kw, vw, down, up_all, shared_out, outgoing, recv,
-    rs_send, rs_recv, acc, rank_part, rank_in, ret_send, ret_recv,
-    load_sem, idx_send_sem, idx_recv_sem, up_send_sem, up_recv_sem, v_send_sem, v_recv_sem,
+    rs_send, rs_recv, acc, flag, rank_part, rank_in, direct_in, ret_send, ret_recv,
+    load_sem, store_sem, x_send_sem, x_recv_sem, idx_send_sem, idx_recv_sem, up_send_sem, up_recv_sem, v_send_sem, v_recv_sem,
     d_send_sem, d_recv_sem, rs_send_sem, rs_recv_sem, p_send_sem, p_recv_sem, r_send_sem, r_recv_sem,
 ):
     me = lax.axis_index("aa")
     mb = lax.axis_index("ba")
     rows = tok.shape[0]
-    kv = keys.shape[1]
+    kv = acc.shape[1] // 2
     half = n // 2
     slots = direct + shared
     groups = LANES // twice_rank
@@ -351,17 +351,6 @@
     count = jnp.int32
 
     barrier = pltpu.get_barrier_semaphore()
-
-    def greet_aa(i, _):
-        pl.semaphore_signal(barrier, inc=1, device_id={"aa": lax.rem(me + i, n)}, device_id_type=MESH)
-        return 0
-
-    def greet_ba(i, _):
-        pl.semaphore_signal(barrier, inc=1, device_id={"ba": lax.rem(mb + i, m)}, device_id_type=MESH)
-        return 0
-
-    lax.fori_loop(1, n, greet_aa, 0)
-    lax.fori_loop(1, m, greet_ba, 0)
 
     loads = [
         pltpu.make_async_copy(idx_hbm, idx_mine, load_sem.at[0]),
@@ -373,8 +362,8 @@
         pltpu.make_async_copy(vw_hbm, vw, load_sem.at[4]),
         pltpu.make_async_copy(down_hbm, down, load_sem.at[5]),
     ]
-    for c in loads:
-        c.start()
+    for at in (0, 2, 1, 3, 4, 5):
+        loads[at].start()
 
     def partner(mask):
         other = me
@@ -382,6 +371,20 @@
             other = jnp.where(lax.rem(mask // b, 2) == 1, xor_bit(other, b), other)
         return other
 
+    def greet_aa(i, _):
+        pl.semaphore_signal(barrier, inc=1, device_id={"aa": lax.rem(me + i, n)}, device_id_type=MESH)
+        return 0
+
+    def greet_ba(i, _):
+        other = lax.rem(mb + i, m)
+        pl.semaphore_signal(barrier, inc=1, device_id={"ba": other}, device_id_type=MESH)
+        there = {"aa": partner(half + 1), "ba": other}
+        pl.semaphore_signal(barrier, inc=1, device_id=there, device_id_type=MESH)
+        return 0
+
+    lax.fori_loop(1, n, greet_aa, 0)
+    lax.fori_loop(1, m, greet_ba, 0)
+
     def chosen(masks, t):
         return sum([jnp.where(t == at, mask, 0) for at, mask in enumerate(masks)], jnp.int32(0))
 
@@ -392,22 +395,47 @@
             device_id={"aa": partner(mask)}, device_id_type=MESH,
         )
 
-    def up_copy(mask):
-        hop = low_bit(mask)
-        return pltpu.make_async_remote_copy(
-            src_ref=up_all.at[mask - hop], dst_ref=up_all.at[mask],
-            send_sem=up_send_sem.at[mask], recv_sem=up_recv_sem.at[mask],
-            device_id={"aa": xor_bit(me, hop)}, device_id_type=MESH,
-        )
-
-    def shared_copy(mask):
-        hop = low_bit(mask)
-        source = shared_out if mask == half else recv.at[mask - hop, pl.ds(direct, shared)]
-        return pltpu.make_async_remote_copy(
-            src_ref=source, dst_ref=recv.at[mask, pl.ds(direct, shared)],
-            send_sem=v_send_sem.at[mask], recv_sem=v_recv_sem.at[mask],
-            device_id={"aa": xor_bit(me, hop)}, device_id_type=MESH,
-        )
+    side = half // 2
+    inner = lax.rem(me // half + me // side, 2) == 1
+    outer = jnp.logical_not(inner)
+    across = half + side
+
+    def up_copy(at, source, target, mask):
+        return pltpu.make_async_remote_copy(
+            src_ref=up_all.at[source], dst_ref=up_all.at[target],
+            send_sem=up_send_sem.at[at], recv_sem=up_recv_sem.at[target],
+            device_id={"aa": partner(mask)}, device_id_type=MESH,
+        )
+
+    own_across = (0, 0, across, across)
+    own_side = (1, 0, side, side)
+    own_pair = (2, 0, 1, 1)
+    pair_copies = {q: (3 + q // side, q, q + 1, 1) for q in (side, half, across)}
+    line_copies = {side: (7, side, half, across), across: (8, across, half, side), half: (9, half, across, side)}
+
+    def up_arrived(target):
+        up_copy(0, 0, target, target).wait_recv()
+
+    def shared_copy(at, source, target, mask):
+        return pltpu.make_async_remote_copy(
+            src_ref=source, dst_ref=recv.at[target, pl.ds(direct, shared)],
+            send_sem=v_send_sem.at[at], recv_sem=v_recv_sem.at[target],
+            device_id={"aa": partner(mask)}, device_id_type=MESH,
+        )
+
+    nearest = jnp.where(inner, across, half)
+
+    def shared_first():
+        return shared_copy(0, shared_out, nearest, nearest)
+
+    def shared_line(q):
+        return shared_copy(1 + (q == half), recv.at[q, pl.ds(direct, shared)], across + half - q, side)
+
+    def shared_pair(q):
+        return shared_copy(3 + (q == half), recv.at[q, pl.ds(direct, shared)], q + 1, 1)
+
+    def shared_arrived(q):
+        shared_copy(0, shared_out, q, q).wait_recv()
 
     def row_copy(mask, height):
         return pltpu.make_async_remote_copy(
@@ -415,9 +443,6 @@
             send_sem=d_send_sem.at[mask], recv_sem=d_recv_sem.at[mask],
             device_id={"aa": partner(mask)}, device_id_type=MESH,
         )
-
-    def hops_below(mask):
-        return [b for b in bits if b < low_bit(mask)]
 
     earlier = lax.broadcasted_iota(count, (rows, rows), 0)
     later = lax.broadcasted_iota(count, (rows, rows), 1)
@@ -445,41 +470,36 @@
     def fill(bank, height):
         return gathered(lax.broadcasted_iota(count, (height, rows), 0) + bank * stride, code_row)
 
-    pl.semaphore_wait(barrier, n + m - 2)
+    loads[2].wait()
+    shared_out[...] = gathered(lax.broadcasted_iota(count, (shared, rows), 0), shared_row)
+    pl.semaphore_wait(barrier, n - 1 + 2 * (m - 1))
 
     def send_idx(mask, _):
         idx_copy(mask, me).start()
         return 0
 
     lax.fori_loop(1, n, send_idx, 0)
+    shared_first().start()
     loads[1].wait()
-    for b in bits:
-        if b != half // 2:
-            up_copy(b).start()
-    loads[2].wait()
-    shared_out[...] = gathered(lax.broadcasted_iota(count, (shared, rows), 0), shared_row)
-    shared_copy(half).start()
-    if half > 1:
-        up_copy(half // 2).start()
-
-    near = sorted(range(1, half), key=lambda mask: (-low_bit(mask) * 0 - mask // 2, mask))
-    far = sorted(range(half, n), key=lambda mask: (mask % 2, mask))
-
-    def send_near(t, _):
-        mask = chosen(near, t)
+
+    @pl.when(inner)
+    def _():
+        up_copy(*own_across).start()
+
+    up_copy(*own_side).start()
+
+    def send_near(mask, _):
         outgoing[mask] = fill(partner(mask), near_rows)
         row_copy(mask, near_rows).start()
         return 0
 
-    def send_far(t, _):
-        mask = chosen(far, t)
+    def send_far(mask, _):
         outgoing[mask, pl.ds(0, direct)] = fill(partner(mask), direct)
         row_copy(mask, direct).start()
         return 0
 
-    lax.fori_loop(0, len(near), send_near, 0)
-    first = len(far) // 2
-    lax.fori_loop(0, first, send_far, 0)
+    lax.fori_loop(side, side + 1, send_near, 0)
+    lax.fori_loop(1, 2, send_near, 0)
 
     def rs_copy(q):
         hop = low_bit(q)
@@ -541,9 +561,9 @@
     over_ranks = jnp.dot(padded.astype(BF16), tri[...], preferred_element_type=F32)[:n].astype(count)
     place = jnp.where(over_all > 0.5, direct + over_ranks, place)
     excess = jnp.where(place >= jnp.where(far_all, slots, near_rows), 1, 0)
-    flag[...] = jnp.broadcast_to(
-        jnp.max(jnp.max(excess, axis=1, keepdims=True), axis=0, keepdims=True), flag.shape
-    )
+    flag[0] = jnp.max(excess)
+    flag_copy = pltpu.make_async_copy(flag, flag_hbm, store_sem.at[0])
+    flag_copy.start()
     to_me = jnp.where(banks == me, place, -1)
     for s in range(n):
         mine[s] = to_me[s:s + 1]
@@ -569,6 +589,16 @@
             send_sem=p_send_sem.at[b, mask], recv_sem=p_recv_sem.at[b, mask],
             device_id={"ba": lax.rem(mb + b + 1, m)}, device_id_type=MESH,
         )
+
+    def direct_copy(b):
+        return pltpu.make_async_remote_copy(
+            src_ref=rank_part.at[half + 1], dst_ref=direct_in.at[b],
+            send_sem=x_send_sem.at[b], recv_sem=x_recv_sem.at[b],
+            device_id={"aa": partner(half + 1), "ba": lax.rem(mb + b, m)}, device_id_type=MESH,
+        )
+
+    def goes_direct(mask):
+        return mask == half + 1
 
     def ret_copy(mask):
         return pltpu.make_async_remote_copy(
@@ -602,8 +632,16 @@
         for g in range(1, groups):
             together = jnp.where(lane == g, total[g * packed:(g + 1) * packed], together)
         rank_part[mask] = together
-        for b in range(m - 1):
-            part_copy(b, mask).start()
+
+        @pl.when(jnp.logical_not(goes_direct(mask) & outer))
+        def _():
+            for b in range(m - 1):
+                part_copy(b, mask).start()
+
+        @pl.when(goes_direct(mask) & outer)
+        def _():
+            for b in range(m):
+                direct_copy(b).start()
 
     def finish(mask):
         total = rank_part[mask]
@@ -621,9 +659,17 @@
             ret_copy(mask).start()
 
     def final(mask):
-        @pl.when(mask > 0)
+        @pl.when((mask > 0) & jnp.logical_not(goes_direct(mask) & inner))
         def _():
             ret_copy(mask).wait_recv()
+
+        @pl.when(goes_direct(mask) & inner)
+        def _():
+            total = jnp.zeros((packed, LANES), F32)
+            for b in range(m):
+                direct_copy(b).wait_recv()
+                total = total + direct_in[b]
+            ret_recv[half + 1] = total
 
         bank = partner(mask)
         together = ret_recv[mask]
@@ -647,73 +693,140 @@
             pick, lo, preferred_element_type=F32
         )
 
-    order = [0] + sorted(range(1, half), key=lambda mask: (mask // 2, mask)) + far
     loads[5].wait()
 
-    def relay_up(mask):
-        up_copy(mask).wait_recv()
-        for b in hops_below(mask):
-            up_copy(mask + b).start()
-
-    def relay_shared(mask):
-        shared_copy(mask).wait_recv()
-        for b in hops_below(mask):
-            shared_copy(mask + b).start()
-
-    def step(t, _):
-        @pl.when((t >= 1) & (t < n + 1))
-        def _():
-            finish(chosen(order, t - 1))
-
-        for at, mask in enumerate(order):
-            if mask and mask != half and mask % 2 == 0 or mask > half:
-                @pl.when(t == at)
-                def _():
-                    if mask % 2 == 0:
-                        relay_up(mask)
-                    if mask > half:
-                        relay_shared(mask)
-
-        @pl.when(t == 2)
-        def _():
-            for b in ba_bits:
-                rs_copy(b).wait_recv()
-                rs_send[0] += rs_recv[b]
-            acc[...] = rs_send[0]
-
-        @pl.when(t >= 2)
-        def _():
-            for at, mask in enumerate(order):
-                if mask % 2:
-                    @pl.when(t == at + 2)
-                    def _():
-                        up_copy(mask).wait_recv()
-
-            final(chosen(order, t - 2))
-
-        @pl.when(t < n)
-        def _():
-            partial(chosen(order, t))
-
-        return 0
-
-    lax.fori_loop(0, 2, step, 0)
-    relay_up(half)
-    lax.fori_loop(first, len(far) - 1, send_far, 0)
-    relay_shared(half)
-    lax.fori_loop(len(far) - 1, len(far), send_far, 0)
-    lax.fori_loop(2, n + 2, step, 0)
-    keys[...] = acc[:, :kv].astype(BF16)
-    values[...] = acc[:, kv:].astype(BF16)
-
-    for mask in range(1, n):
-        up_copy(mask).wait_send()
-    for mask in range(half, n):
-        shared_copy(mask).wait_send()
+    def line_up(q):
+        up_arrived(q)
+
+        @pl.when(inner)
+        def _():
+            up_copy(*line_copies[q]).start()
+
+    def pair_up(q):
+        up_copy(*pair_copies[q]).start()
+
+    def pair_shared(q):
+        shared_arrived(q)
+        shared_pair(q).start()
+
+    def init():
+        for b in ba_bits:
+            rs_copy(b).wait_recv()
+            rs_send[0] += rs_recv[b]
+        acc[...] = rs_send[0]
+
+    two, three, four, five, six, seven = side, side + 1, half, half + 1, across, across + 1
+    inner_turns = [
+        (0, 0), (0, 1),
+        (0, two), (0, four), (0, five), (1, 0), (2, 0), (1, 1), (1, two), (1, four), (1, five), (3, four),
+        (0, three), (0, six), (1, three), (0, seven), (1, six), (2, 1), (1, seven), (3, five), (2, two), (2, three),
+        (2, six), (2, seven), (2, four), (2, five),
+    ]
+    outer_turns = [
+        (0, 0), (0, 1),
+        (0, two), (1, 0), (2, 0), (1, 1), (1, two), (0, three), (0, six), (1, three), (0, seven), (1, six),
+        (2, 1), (1, seven), (2, two), (2, four), (0, four), (2, three), (1, four), (2, five), (2, six), (0, five),
+        (2, seven), (4, 0), (4, 0), (4, 0),
+    ]
+    opening = 2
+
+    def turn(t, _):
+        kind = jnp.where(inner, chosen([k for k, _ in inner_turns], t), chosen([k for k, _ in outer_turns], t))
+        mask = jnp.where(inner, chosen([q for _, q in inner_turns], t), chosen([q for _, q in outer_turns], t))
+
+        @pl.when((kind == 1) & (mask == 0) & outer)
+        def _():
+            pair_shared(across)
+            pair_shared(half)
+
+        for q in (half + 1, across + 1):
+            @pl.when((kind == 0) & (mask == q))
+            def _():
+                shared_arrived(q)
+
+        @pl.when((kind == 1) & (mask == jnp.where(inner, half, side + 1)))
+        def _():
+            line_up(half)
+            pair_up(half)
+
+        @pl.when((kind == 2) & (mask == 1) & outer)
+        def _():
+            line_up(across)
+            pair_up(across)
+
+        @pl.when((kind == 2) & (mask == 0))
+        def _():
+            init()
+
+        for q in range(1, n, 2):
+            @pl.when((kind == 2) & (mask == q))
+            def _():
+                up_arrived(q)
+
+        @pl.when(kind == 0)
+        def _():
+            partial(mask)
+
+        @pl.when(kind == 1)
+        def _():
+            finish(mask)
+
+        @pl.when(kind == 2)
+        def _():
+            final(mask)
+
+        @pl.when(kind == 3)
+        def _():
+            send_far(mask, 0)
+
+        return 0
+
+    @pl.when(inner)
+    def _():
+        for q in (half, across):
+            shared_arrived(q)
+            shared_line(q).start()
+            shared_pair(q).start()
+
+    line_up(side)
+    lax.fori_loop(0, 2, lambda t, _: send_far(nearest + t, 0), 0)
+    lax.fori_loop(side + 1, side + 2, send_near, 0)
+
+    @pl.when(outer)
+    def _():
+        lax.fori_loop(across, across + 2, send_far, 0)
+
+    up_copy(*own_pair).start()
+    pair_up(side)
+    lax.fori_loop(0, opening, turn, 0)
+
+    @pl.when(inner)
+    def _():
+        line_up(across)
+        pair_up(across)
+
+    lax.fori_loop(opening, len(inner_turns), turn, 0)
+    out[...] = acc[...].astype(BF16)
+
+    shared_first().wait_send()
+    for copy in (own_side, own_pair, *pair_copies.values()):
+        up_copy(*copy).wait_send()
+    for q in (half, across):
+        shared_pair(q).wait_send()
+
+    @pl.when(inner)
+    def _():
+        for copy in (own_across, *line_copies.values()):
+            up_copy(*copy).wait_send()
+        for q in (half, across):
+            shared_line(q).wait_send()
 
     def drain(mask, _):
         idx_copy(mask, me).wait_send()
-        ret_copy(mask).wait_send()
+
+        @pl.when(jnp.logical_not(goes_direct(mask) & outer))
+        def _():
+            ret_copy(mask).wait_send()
 
         @pl.when(mask < half)
         def _():
@@ -728,13 +841,23 @@
     lax.fori_loop(1, n, drain, 0)
 
     def drain_parts(mask, _):
-        for b in range(m - 1):
-            part_copy(b, mask).wait_send()
+        @pl.when(jnp.logical_not(goes_direct(mask) & outer))
+        def _():
+            for b in range(m - 1):
+                part_copy(b, mask).wait_send()
+
         return 0
 
     lax.fori_loop(0, n, drain_parts, 0)
+
+    @pl.when(outer)
+    def _():
+        for b in range(m):
+            direct_copy(b).wait_send()
+
     for q in range(1, m):
         rs_copy(q).wait_send()
+    flag_copy.wait()
 
 
 def packed_call(n, m, cap, idx, tokens, key_weight, value_weight, down_flat, up_flat, resident):
@@ -744,7 +867,7 @@
     kv_width = key_weight.shape[1]
     kv = kv_width // m
     direct = rows // n
-    shared = 3 * direct // 4
+    shared = 5 * direct // 8
     near_rows = 3 * direct // 2
     slots = direct + shared
     stride = resident * cap
@@ -753,12 +876,11 @@
     return pl.pallas_call(
         functools.partial(packed_kernel, n, m, direct, shared, near_rows, stride, resident, twice_rank),
         out_shape=[
-            jax.ShapeDtypeStruct((rows, kv), BF16),
-            jax.ShapeDtypeStruct((rows, kv), BF16),
-            jax.ShapeDtypeStruct((8, LANES), jnp.int32),
+            jax.ShapeDtypeStruct((rows, 2 * kv), BF16),
+            jax.ShapeDtypeStruct((1,), jnp.int32),
         ],
-        in_specs=[pl.BlockSpec(memory_space=pl.ANY)] * 6,
-        out_specs=[pl.BlockSpec(memory_space=pltpu.VMEM)] * 3,
+        in_specs=[pl.BlockSpec(memory_space=pltpu.HBM)] * 6,
+        out_specs=[pl.BlockSpec(memory_space=pltpu.VMEM), pl.BlockSpec(memory_space=pltpu.HBM)],
         scratch_shapes=[
             pltpu.VMEM((1, rows), jnp.int32),
             pltpu.VMEM((n, 1, rows), jnp.int32),
@@ -775,19 +897,21 @@
             pltpu.VMEM((m, rows, 2 * kv), F32),
             pltpu.VMEM((m, rows, 2 * kv), F32),
             pltpu.VMEM((rows, 2 * kv), F32),
+            pltpu.SMEM((1,), jnp.int32),
             pltpu.VMEM((n, packed, LANES), F32),
             pltpu.VMEM((m - 1, n, packed, LANES), F32),
+            pltpu.VMEM((m, packed, LANES), F32),
             pltpu.VMEM((n, packed, LANES), F32),
             pltpu.VMEM((n, packed, LANES), F32),
-            dma((6,)),
-            dma((n,)), dma((n,)), dma((n,)), dma((n,)), dma((n,)), dma((n,)),
+            dma((6,)), dma((1,)), dma((m,)), dma((m,)),
+            dma((n,)), dma((n,)), dma((10,)), dma((n,)), dma((5,)), dma((n,)),
             dma((n,)), dma((n,)),
             dma((m,)), dma((m,)),
             dma((m - 1, n)), dma((m - 1, n)),
             dma((n,)), dma((n,)),
         ],
         compiler_params=pltpu.CompilerParams(
-            collective_id=1, has_side_effects=True, vmem_limit_bytes=56 * 1024 * 1024
+            collective_id=1, has_side_effects=True, vmem_limit_bytes=63 * 1024 * 1024
         ),
     )(idx, tokens, key_weight, value_weight, down_flat, up_flat)
 
@@ -815,7 +939,7 @@
         total = pl.pallas_call(
             functools.partial(kernel, n, m, cap, resident, twice_rank),
             out_shape=jax.ShapeDtypeStruct((rows, 2 * kv), F32),
-            in_specs=[pl.BlockSpec(memory_space=pltpu.VMEM)] + [pl.BlockSpec(memory_space=pl.ANY)] * 5,
+            in_specs=[pl.BlockSpec(memory_space=pltpu.VMEM)] + [pl.BlockSpec(memory_space=pltpu.HBM)] * 5,
             out_specs=pl.BlockSpec(memory_space=pltpu.VMEM),
             scratch_shapes=[
                 pltpu.VMEM((rows, width), BF16),
@@ -843,12 +967,14 @@
         )(
             *operands,
         )
-        return total[:, :kv].astype(BF16), total[:, kv:].astype(BF16)
-
-    if rows % (64 * n) or 7 * rows // (4 * n) >= chunk:
-        return any_load()
-    keys, values, flag = packed_call(n, m, cap, *operands, resident)
-    return lax.cond(flag[0, 0] > 0, any_load, lambda: (keys, values))
+        return total.astype(BF16)
+
+    if n // 2 != 4 or rows % (64 * n) or 13 * rows // (8 * n) >= chunk:
+        both = any_load()
+    else:
+        both, flag = packed_call(n, m, cap, *operands, resident)
+        both = lax.cond(flag.reshape(()) > 0, any_load, lambda: both)
+    return both[:, :kv], both[:, kv:]
 
 
 def solution(mesh):

time: 104 us -> 85.3 us (0.82); the launches traced: 102 us -> 85.2 us
  Pallas kernels: 97.6 us -> 82.9 us
  local copies, waits for them, and re-layouts: 2.62 us -> 0.83 us
    pallas_call x1, Pallas kernels: 97.6 us -> 82.9 us  [packed_call(): pl.pallas_call(functools.partial(packed_kernel, n, m, direct, shared, nea...]
    unnamed x10 -> x2, local copies, waits for them, and re-layouts: 1.42 us -> 0.01 us
where the time goes in v2:
time: 85.3 us; the launch traced here: 85.2 us
  Pallas kernels  82.9 us (97%)
  between operations  1.28 us (2%)
    pallas_call x1, Pallas kernels, packed_call(): pl.pallas_call(functools.partial(packed_kernel, n, m, direct, shared, nea...  82.9 us

profile of v2, /device:TPU:11, one launch (start us, length us, event | category | flops | bytes accessed | tf_op | source)
XLA Modules:
  0.0 85.2 jit_solution(5717242054977587156)
XLA Ops:
  0.6 0.0 copy-start
  0.6 82.9 %shard_map.77 = (bf16[512,512]{1,0:T(8,128)(2,1)S(1)}, s32[1]{0:T(128)}) custom-call(s32[1,512]{1,0:T(1,128)} %bitcast.8, bf16[512,2048]{1,0:T(8,128)(2,1)} %tok_hbm.1, bf16[2048,1024]{1,0:T(8,128)(2,1)} %kw_hbm.1, bf16[2048,1024]{1,0:T(8,128)(2,1)} %vw_hbm.1, bf16[512,2048]{1,0:T(8,128)(2,1)} %bitcast.4, bf16[512,1024]{1,0:T(8,128)(2,1)} %bitcast.6), custom_call_target="tpu_custom_call" | custom-call | tf_op jit(solution)/shard_map/pallas_call | solution.py:876
  84.1 0.0 copy-done
  84.2 0.2 conditional.1
  84.3 0.8 fusion
Async XLA Ops:
  0.6 83.5 %copy-start = (s32[512,1]{0,1:T(1,128)S(1)}, s32[512,1]{0,1:T(1,128)}, u32[]{:S(2)}) copy-start(s32[512,1]{0,1:T(1,128)} %param.9) | copy-start | bytes 6148

commit v3 on v2

--- a/solution.py
+++ b/solution.py
@@ -331,7 +331,7 @@
     n, m, direct, shared, near_rows, stride, resident, twice_rank,
     idx_hbm, tok_hbm, kw_hbm, vw_hbm, down_hbm, up_hbm,
     out, flag_hbm,
-    idx_mine, idx_all, mine, tri, tok, kw, vw, down, up_all, shared_out, outgoing, recv,
+    idx_mine, idx_all, mine, tri, tok, kw, vw, down, down_t, up_all, shared_out, outgoing, recv,
     rs_send, rs_recv, acc, flag, rank_part, rank_in, direct_in, ret_send, ret_recv,
     load_sem, store_sem, x_send_sem, x_recv_sem, idx_send_sem, idx_recv_sem, up_send_sem, up_recv_sem, v_send_sem, v_recv_sem,
     d_send_sem, d_recv_sem, rs_send_sem, rs_recv_sem, p_send_sem, p_recv_sem, r_send_sem, r_recv_sem,
@@ -388,10 +388,13 @@
     def chosen(masks, t):
         return sum([jnp.where(t == at, mask, 0) for at, mask in enumerate(masks)], jnp.int32(0))
 
+    def landed(ref, sem):
+        pltpu.make_async_copy(ref, ref, sem).wait()
+
     def idx_copy(mask, source):
         return pltpu.make_async_remote_copy(
             src_ref=idx_mine, dst_ref=idx_all.at[source],
-            send_sem=idx_send_sem.at[mask], recv_sem=idx_recv_sem.at[mask],
+            send_sem=idx_send_sem.at[0], recv_sem=idx_recv_sem.at[0],
             device_id={"aa": partner(mask)}, device_id_type=MESH,
         )
 
@@ -541,11 +544,7 @@
     for mask in range(half):
         recv[mask, pl.ds(near_rows, slots - near_rows)] = jnp.zeros((slots - near_rows, tok.shape[1]), BF16)
 
-    def wait_idx(mask, _):
-        idx_copy(mask, partner(mask)).wait_recv()
-        return 0
-
-    lax.fori_loop(1, n, wait_idx, 0)
+    landed(idx_all.at[pl.ds(0, n - 1)], idx_recv_sem.at[0])
     everyone = jnp.concatenate([idx_all[s] for s in range(n)], axis=0)
     banks = everyone // resident
     matches = [banks == b for b in range(n)]
@@ -585,15 +584,15 @@
 
     def part_copy(b, mask):
         return pltpu.make_async_remote_copy(
-            src_ref=rank_part.at[mask], dst_ref=rank_in.at[b, mask],
-            send_sem=p_send_sem.at[b, mask], recv_sem=p_recv_sem.at[b, mask],
+            src_ref=rank_part.at[mask], dst_ref=rank_in.at[mask, b],
+            send_sem=p_send_sem.at[mask], recv_sem=p_recv_sem.at[mask],
             device_id={"ba": lax.rem(mb + b + 1, m)}, device_id_type=MESH,
         )
 
     def direct_copy(b):
         return pltpu.make_async_remote_copy(
             src_ref=rank_part.at[half + 1], dst_ref=direct_in.at[b],
-            send_sem=x_send_sem.at[b], recv_sem=x_recv_sem.at[b],
+            send_sem=x_send_sem.at[0], recv_sem=x_recv_sem.at[0],
             device_id={"aa": partner(half + 1), "ba": lax.rem(mb + b, m)}, device_id_type=MESH,
         )
 
@@ -617,9 +616,7 @@
             row_copy(mask, direct).wait_recv()
 
         source = partner(mask)
-        wide = lax.dot_general(
-            recv[mask], down[...], (((1,), (1,)), ((), ())), preferred_element_type=F32
-        )
+        wide = jnp.dot(recv[mask], down_t[...], preferred_element_type=F32)
         own = owned(lax.broadcasted_iota(count, (slots, rows), 0), mine[source], idx_all[source])
         wide = jnp.where(own, wide, 0.0)
         total = wide[:, :LANES]
@@ -645,9 +642,9 @@
 
     def finish(mask):
         total = rank_part[mask]
+        landed(rank_in.at[mask], p_recv_sem.at[mask])
         for b in range(m - 1):
-            part_copy(b, mask).wait_recv()
-            total = total + rank_in[b, mask]
+            total = total + rank_in[mask, b]
 
         @pl.when(mask == 0)
         def _():
@@ -666,8 +663,8 @@
         @pl.when(goes_direct(mask) & inner)
         def _():
             total = jnp.zeros((packed, LANES), F32)
+            landed(direct_in, x_recv_sem.at[0])
             for b in range(m):
-                direct_copy(b).wait_recv()
                 total = total + direct_in[b]
             ret_recv[half + 1] = total
 
@@ -693,7 +690,6 @@
             pick, lo, preferred_element_type=F32
         )
 
-    loads[5].wait()
 
     def line_up(q):
         up_arrived(q)
@@ -798,6 +794,14 @@
 
     up_copy(*own_pair).start()
     pair_up(side)
+    loads[5].wait()
+
+    def turn_down(c, _):
+        strip = pl.ds(pl.multiple_of(c * LANES * 2, LANES), LANES * 2)
+        down_t[strip] = down[:, strip].T
+        return 0
+
+    lax.fori_loop(0, down.shape[1] // (2 * LANES), turn_down, 0)
     lax.fori_loop(0, opening, turn, 0)
 
     @pl.when(inner)
@@ -821,9 +825,9 @@
         for q in (half, across):
             shared_line(q).wait_send()
 
+    landed(idx_all.at[pl.ds(0, n - 1)], idx_send_sem.at[0])
+
     def drain(mask, _):
-        idx_copy(mask, me).wait_send()
-
         @pl.when(jnp.logical_not(goes_direct(mask) & outer))
         def _():
             ret_copy(mask).wait_send()
@@ -843,8 +847,7 @@
     def drain_parts(mask, _):
         @pl.when(jnp.logical_not(goes_direct(mask) & outer))
         def _():
-            for b in range(m - 1):
-                part_copy(b, mask).wait_send()
+            landed(rank_in.at[mask], p_send_sem.at[mask])
 
         return 0
 
@@ -852,8 +855,7 @@
 
     @pl.when(outer)
     def _():
-        for b in range(m):
-            direct_copy(b).wait_send()
+        landed(direct_in, x_send_sem.at[0])
 
     for q in range(1, m):
         rs_copy(q).wait_send()
@@ -890,6 +892,7 @@
             pltpu.VMEM((width, kv_width), BF16),
             pltpu.VMEM((width, kv_width), BF16),
             pltpu.VMEM((flat, width), BF16),
+            pltpu.VMEM((width, flat), BF16),
             pltpu.VMEM((n, flat, kv), BF16),
             pltpu.VMEM((shared, width), BF16),
             pltpu.VMEM((n, near_rows, width), BF16),
@@ -899,15 +902,15 @@
             pltpu.VMEM((rows, 2 * kv), F32),
             pltpu.SMEM((1,), jnp.int32),
             pltpu.VMEM((n, packed, LANES), F32),
-            pltpu.VMEM((m - 1, n, packed, LANES), F32),
+            pltpu.VMEM((n, m - 1, packed, LANES), F32),
             pltpu.VMEM((m, packed, LANES), F32),
             pltpu.VMEM((n, packed, LANES), F32),
             pltpu.VMEM((n, packed, LANES), F32),
-            dma((6,)), dma((1,)), dma((m,)), dma((m,)),
-            dma((n,)), dma((n,)), dma((10,)), dma((n,)), dma((5,)), dma((n,)),
+            dma((6,)), dma((1,)), dma((1,)), dma((1,)),
+            dma((1,)), dma((1,)), dma((10,)), dma((n,)), dma((5,)), dma((n,)),
             dma((n,)), dma((n,)),
             dma((m,)), dma((m,)),
-            dma((m - 1, n)), dma((m - 1, n)),
+            dma((n,)), dma((n,)),
             dma((n,)), dma((n,)),
         ],
         compiler_params=pltpu.CompilerParams(

time: 85.3 us -> 84.5 us (level)
  no operation moved by 1% of the time
where the time goes in v3:
time: 84.5 us; the launch traced here: 84.4 us
  Pallas kernels  82.1 us (97%)
  between operations  1.28 us (2%)
    pallas_call x1, Pallas kernels, packed_call(): pl.pallas_call(functools.partial(packed_kernel, n, m, direct, shared, nea...  82.1 us

profile of v3, /device:TPU:11, one launch (start us, length us, event | category | flops | bytes accessed | tf_op | source)
XLA Modules:
  0.0 84.4 jit_solution(8242562478758691004)
XLA Ops:
  0.6 0.0 copy-start
  0.6 82.1 %shard_map.77 = (bf16[512,512]{1,0:T(8,128)(2,1)S(1)}, s32[1]{0:T(128)}) custom-call(s32[1,512]{1,0:T(1,128)} %bitcast.8, bf16[512,2048]{1,0:T(8,128)(2,1)} %tok_hbm.1, bf16[2048,1024]{1,0:T(8,128)(2,1)} %kw_hbm.1, bf16[2048,1024]{1,0:T(8,128)(2,1)} %vw_hbm.1, bf16[512,2048]{1,0:T(8,128)(2,1)} %bitcast.4, bf16[512,1024]{1,0:T(8,128)(2,1)} %bitcast.6), custom_call_target="tpu_custom_call" | custom-call | tf_op jit(solution)/shard_map/pallas_call | solution.py:878
  83.3 0.0 copy-done
  83.3 0.2 conditional.1
  83.5 0.8 fusion
Async XLA Ops:
  0.6 82.7 %copy-start = (s32[512,1]{0,1:T(1,128)S(1)}, s32[512,1]{0,1:T(1,128)}, u32[]{:S(2)}) copy-start(s32[512,1]{0,1:T(1,128)} %param.9) | copy-start | bytes 6148
